TPU v7x, 32 devices: a whole 2x2x4 slice. The times are simulated.
32 devices in a mesh: blk: 2 (over x), wide: 16 (over z, y, core).
Axes of the slice: x: 2, y: 2, z: 4, core: 2. Of those that a mesh axis runs over, the one named last changes fastest.
Arguments:
- volume: float32 [2, 2, 512, 896], P('blk', None, 'wide'), may hold values from -1.6 to 1.6
- path_lengths: float32 [2, 2, 2], replicated, may hold values from 0.5 to 2
- probe: float32 [2, 128, 128], replicated, may hold values from -6 to 6
- measured: bfloat16 [2, 16, 14, 128, 128], P('blk', 'wide'), may hold values from 0.19921875 to 3
- jitter: int32 [2, 2, 16, 14], P(None, 'blk', 'wide'), may hold values from 0 to 15
- step_sizes: float32 [2], replicated, may hold values from 0.02 to 0.2
Outputs:
- new_volume: float32 [2, 2, 512, 896], P('blk', None, 'wide')
- misfit: float32 [], replicated
All inputs are finite; a program needn't handle non-finite values.
Results may differ from a plain program's by a relative error of at most 0.0003.
Values sent between devices are 32-bit elements; how exact they have to be, the bound alone decides.
A program may use at most 64 MiB of HBM per device.

v0:
```python
import math

import jax
import jax.numpy as jnp
from jax import lax
from jax.sharding import PartitionSpec as P

ROWS_DEV = 32
PATCH = 128
CSTEP = 64


highest = lax.Precision.HIGHEST
floor_value = 0.25


def passed_along(value, axis, steps):
    count = lax.axis_size(axis)
    pairs = [(source, (source + steps) % count) for source in range(count)]
    return lax.ppermute(value, axis, pairs)


def from_behind(shard, axis, by):
    count = lax.axis_size(axis)
    pairs = [(i, i + by) for i in range(count) if 0 <= i + by < count]
    return lax.ppermute(shard, axis, pairs)


def dft_tables(length):
    grid = jnp.arange(length, dtype=jnp.int32)
    product = grid[:, None] * grid[None, :] % length
    angles = product.astype(jnp.float32) * (2.0 * math.pi / length)
    factor = 1.0 / math.sqrt(length)
    return (jnp.cos(angles) * factor, -jnp.sin(angles) * factor)


def left_apply(table, batch):
    return jnp.einsum("jk,bkl->bjl", table, batch, precision=highest)


def right_apply(batch, table):
    return jnp.einsum("bjk,kl->bjl", batch, table, precision=highest)


def transform(real_in, imag_in, cos_table, sin_table):
    mid_real = left_apply(cos_table, real_in) - left_apply(sin_table, imag_in)
    mid_imag = left_apply(cos_table, imag_in) + left_apply(sin_table, real_in)
    out_real = right_apply(mid_real, cos_table) - right_apply(mid_imag, sin_table)
    out_imag = right_apply(mid_real, sin_table) + right_apply(mid_imag, cos_table)
    return (out_real, out_imag)


def strip_update(
    strip_real,
    strip_imaginary,
    probe,
    measured,
    jitter_rows,
    jitter_cols,
    row_corner,
    column_corner,
):
    patch_len = probe.shape[-1]
    number = measured.shape[0]
    cos_table, sin_table = dft_tables(patch_len)
    starts_row = row_corner + jitter_rows
    starts_col = column_corner + CSTEP * jnp.arange(number, dtype=jnp.int32) + jitter_cols

    def window(image, top, left):
        return lax.dynamic_slice(image, (top, left), (patch_len, patch_len))

    pick = jax.vmap(window, in_axes=(None, 0, 0))
    obj_real = pick(strip_real, starts_row, starts_col)
    obj_imag = pick(strip_imaginary, starts_row, starts_col)
    probe_real = probe[0]
    probe_imag = probe[1]
    wave_real = probe_real * obj_real - probe_imag * obj_imag
    wave_imag = probe_real * obj_imag + probe_imag * obj_real
    far_real, far_imag = transform(wave_real, wave_imag, cos_table, sin_table)
    modulus = jnp.sqrt(far_real * far_real + far_imag * far_imag)
    target = measured.astype(jnp.float32)
    error = modulus - target
    partial_misfit = jnp.sum(error * error)
    ratio = target / jnp.maximum(modulus, floor_value)
    back_real, back_imag = transform(ratio * far_real, ratio * far_imag, cos_table, -sin_table)
    diff_real = back_real - wave_real
    diff_imag = back_imag - wave_imag
    corr_real = probe_real * diff_real + probe_imag * diff_imag
    corr_imag = probe_real * diff_imag - probe_imag * diff_real

    def place(position, sums):
        acc_real, acc_imag = sums
        top = starts_row[position]
        left = starts_col[position]
        acc_real = lax.dynamic_update_slice(
            acc_real, window(acc_real, top, left) + corr_real[position], (top, left)
        )
        acc_imag = lax.dynamic_update_slice(
            acc_imag, window(acc_imag, top, left) + corr_imag[position], (top, left)
        )
        return (acc_real, acc_imag)

    zeros = jnp.zeros(strip_real.shape, strip_real.dtype)
    acc_real, acc_imag = lax.fori_loop(0, number, place, (zeros, zeros))
    return (acc_real, acc_imag, partial_misfit)


def body(volume, path_lengths, probe, measured, jitter, step_sizes):
    group = lax.axis_index("blk")
    groups = lax.axis_size("blk")
    column = lax.axis_index("wide")
    columns = lax.axis_size("wide")
    slab = volume[0]
    row_len = slab.shape[1]
    col_len = slab.shape[2]
    margin = probe.shape[-1] // 2
    own_paths = lax.dynamic_index_in_dim(path_lengths, group, 1, keepdims=False)

    def slab_term(angle, weight):
        coeffs = lax.dynamic_index_in_dim(own_paths, angle, 0, keepdims=False) * weight
        return jnp.einsum("l,lrc->rc", coeffs, slab, precision=highest)

    def cycle_step(section, carried):
        carried = passed_along(carried, "blk", 1)
        angle = (group - section) % groups
        weight = jnp.where(section < groups, 1.0, 0.0).astype(jnp.float32)
        return carried + slab_term(angle, weight)

    projection = lax.fori_loop(
        1, groups + 1, cycle_step, slab_term(group, jnp.ones((), jnp.float32))
    )
    sources = (2, 1, 0, -1, -2)
    pieces_real = []
    pieces_imag = []
    for offset in sources:
        if offset == 0:
            got_phase = projection
        else:
            got_phase = from_behind(projection, "wide", offset)
        source = column - offset
        valid = ((source >= 0) & (source < columns)).astype(jnp.float32)
        pieces_real.append(jnp.cos(got_phase) * valid)
        pieces_imag.append(jnp.sin(got_phase) * valid)
    ext_real = jnp.concatenate(pieces_real, 0)
    ext_imag = jnp.concatenate(pieces_imag, 0)
    strip_real = jnp.pad(ext_real, ((0, 0), (margin, margin)))
    strip_imaginary = jnp.pad(ext_imag, ((0, 0), (margin, margin)))
    row_corner = ROWS_DEV // 4
    column_corner = PATCH // 4 - ROWS_DEV // 4
    acc_real, acc_imag, local_misfit = strip_update(
        strip_real,
        strip_imaginary,
        probe,
        measured[0, 0],
        jitter[0, 0, 0],
        jitter[1, 0, 0],
        row_corner,
        column_corner,
    )
    acc_real = acc_real[:, margin : margin + col_len]
    acc_imag = acc_imag[:, margin : margin + col_len]

    def rows_of(array, slot):
        return array[slot * row_len : (slot + 1) * row_len]

    total_real = rows_of(acc_real, 2)
    total_imag = rows_of(acc_imag, 2)
    for offset in (-2, -1, 1, 2):
        got_real, got_imag = from_behind(
            (rows_of(acc_real, 2 + offset), rows_of(acc_imag, 2 + offset)), "wide", offset
        )
        total_real = total_real + got_real
        total_imag = total_imag + got_imag
    gradient = rows_of(ext_real, 2) * total_imag - rows_of(ext_imag, 2) * total_real
    total_misfit = lax.psum(local_misfit, ("blk", "wide"))
    scaled = step_sizes[:, None] * own_paths
    coeffs = scaled
    update = jnp.einsum(
        "al,arc->lrc",
        coeffs,
        lax.all_gather(gradient[None], "blk", axis=0, tiled=True),
        precision=highest,
    )
    return ((slab - update)[None], total_misfit)


def solution(mesh):
    in_specs = (
        P("blk", None, "wide", None),
        P(),
        P(),
        P("blk", "wide", None, None, None),
        P(None, "blk", "wide", None),
        P(),
    )
    out_specs = (P("blk", None, "wide", None), P())
    return jax.shard_map(body, mesh=mesh, in_specs=in_specs, out_specs=out_specs, check_vma=False)
```

profile of v0, /device:TPU:0, one launch (start us, length us, event | category | flops | bytes accessed | tf_op | source)
XLA Modules:
  0.0 310.7 jit_solution(9081547119739849727)
XLA Ops:
  3.4 11.1 %while.32 = (s32[]{:T(128)}, f32[32,896]{1,0:T(8,128)S(1)}, s32[]{:T(128)}, f32[2,2]{1,0:T(2,128)S(1)}, f32[2,32,896]{2,1,0:T(8,128)S(1)}, /*index=5*/s32[]{:T(128)}, s32[]{:T(128)}, s32[]{:T(128)}, f32[]{:T(128)}, f32[]{:T(128)}) while((s32[]{:T(128)}, f32[32,896]{1,0:T(8,128)S(1)}, s32[]{:T(128)}, f32[2,2]{1,0:T(2,128)S(1)}, ...), condition=%wide.region_1.2_spmd, body=%wide.region_0.1_spmd.sunk | while | flops 716821 | bytes 1147718 | solution.py:129
  3.4 3.0 collective-permute-start
  7.4 2.2 collective-permute-done
  9.6 1.8 collective-permute-start
  12.4 2.1 collective-permute-done
  14.5 3.7 %collective-permute-start.1 = (f32[32,896]{1,0:T(8,128)S(1)}, f32[32,896]{1,0:T(8,128)S(1)}, u32[]{:S(2)}, u32[]{:S(2)}) collective-permute-start(f32[32,896]{1,0:T(8,128)S(1)} %get-tuple-element.260), channel_id=1, source_target_pairs={{0,2},{1,3},{2,4},{3,5},{4,6},{5,7},{6,8},{7,9},{8,10},{9,11},{10,... | collective-permute-start | bytes 344072 | tf_op jit(solution)/shard_map/ppermute | solution.py:26
  24.9 5.7 %collective-permute-done.4 = f32[32,896]{1,0:T(8,128)S(1)} collective-permute-done((f32[32,896]{1,0:T(8,128)S(1)}, f32[32,896]{1,0:T(8,128)S(1)}, u32[]{:S(2)}, u32[]{:S(2)}) %collective-permute-start.4) | collective-permute-done | bytes 114720 | tf_op jit(solution)/shard_map/ppermute | solution.py:26
  31.4 28.7 %while.34 = (s32[]{:T(128)}, f32[160,1024]{1,0:T(8,128)S(1)}, s32[14,2]{0,1:T(2,128)S(1)}, f32[14,128,128]{2,1,0:T(8,128)S(1)}, s32[]{:T(128)}) while((s32[]{:T(128)}, f32[160,1024]{1,0:T(8,128)S(1)}, s32[14,2]{0,1:T(2,128)S(1)}, f32[14,128,128]{2,1,0:T(8,128)S(1)}, s32[]{:T(128)}) %tuple.120), condition=%wide.while_cond, body=%wide.while_body.sunk | while | flops 2 | bytes 131181 | solution.py:70
  60.3 26.8 %while.35 = (s32[]{:T(128)}, f32[160,1024]{1,0:T(8,128)S(1)}, s32[14,2]{0,1:T(2,128)S(1)}, f32[14,128,128]{2,1,0:T(8,128)S(1)}, s32[]{:T(128)}) while((s32[]{:T(128)}, f32[160,1024]{1,0:T(8,128)S(1)}, s32[14,2]{0,1:T(2,128)S(1)}, f32[14,128,128]{2,1,0:T(8,128)S(1)}, s32[]{:T(128)}) %tuple.127), condition=%wide.while_cond.1, body=%wide.while_body.1.sunk | while | flops 2 | bytes 131181 | solution.py:70
  97.9 2.0 convolution_subtract_fusion.2
  99.9 2.6 fusion.13
  102.5 2.2 fusion.14
  104.7 2.2 fusion.18
  106.9 2.2 fusion.8
  110.9 2.0 fusion.38
  112.9 2.2 fusion.7
  116.8 1.9 multiply_subtract_fusion
  118.9 118.3 %while.33 = (s32[]{:T(128)}, f32[160,1024]{1,0:T(8,128)S(1)}, f32[160,1024]{1,0:T(8,128)S(1)}, s32[14]{0:T(128)S(1)}, s32[14]{0:T(128)S(1)}, /*index=5*/f32[14,1...) while((s32[]{:T(128)}, f32[160,1024]{1,0:T(8,128)S(1)}, ...), condition=%wide.region_3.4_spmd, body=%wide.region_2.3_spmd.sunk | while | flops 32776 | bytes 655581 | solution.py:104
  238.7 3.0 collective-permute-start.11
  241.7 4.4 %collective-permute-start.12 = (f32[32,896]{1,0:T(8,128)S(1)}, f32[32,896]{1,0:T(8,128)S(1)}, u32[]{:S(2)}, u32[]{:S(2)}) collective-permute-start(f32[32,896]{1,0:T(8,128)S(1)} %get-tuple-element.348), channel_id=1, source_target_pairs={{0,2},{1,3},{2,4},{3,5},{4,6},{5,7},{6,8},{7,9},{8,10},{9,11},{10,... | collective-permute-start | bytes 344072 | tf_op jit(solution)/shard_map/ppermute | solution.py:26
  249.0 3.4 %collective-permute-start.7 = (f32[32,896]{1,0:T(8,128)S(1)}, f32[32,896]{1,0:T(8,128)S(1)}, u32[]{:S(2)}, u32[]{:S(2)}) collective-permute-start(f32[32,896]{1,0:T(8,128)S(1)} %get-tuple-element.345), channel_id=1, source_target_pairs={{0,1},{1,2},{2,3},{3,4},{4,5},{5,6},{6,7},{7,8},{8,9},{9,10},{10,1... | collective-permute-start | bytes 344072 | tf_op jit(solution)/shard_map/ppermute | solution.py:26
  252.4 4.3 %collective-permute-start.8 = (f32[32,896]{1,0:T(8,128)S(1)}, f32[32,896]{1,0:T(8,128)S(1)}, u32[]{:S(2)}, u32[]{:S(2)}) collective-permute-start(f32[32,896]{1,0:T(8,128)S(1)} %get-tuple-element.344), channel_id=1, source_target_pairs={{0,2},{1,3},{2,4},{3,5},{4,6},{5,7},{6,8},{7,9},{8,10},{9,11},{10,... | collective-permute-start | bytes 344072 | tf_op jit(solution)/shard_map/ppermute | solution.py:26
  257.9 43.3 %psum.7 = f32[]{:T(128)} all-reduce(f32[]{:T(128)} %get-tuple-element.365), channel_id=1, replica_groups=mesh['blk'=2,'wide'=16] {'blk','wide'}, use_global_device_ids=true, to_apply=%region_5.6 | all-reduce | flops 1 | bytes 8 | tf_op jit(solution)/shard_map/psum | solution.py:175
  301.8 5.8 %all-gather = f32[64,896]{1,0:T(8,128)S(1)} all-gather(f32[32,896]{1,0:T(8,128)S(1)} %multiply_subtract_fusion.2), channel_id=2, replica_groups=mesh['blk'=2,'wide'=16] {'blk'}, dimensions={0}, use_global_device_ids=true | all-gather | bytes 344064 | tf_op jit(solution)/shard_map/all_gather | solution.py:181
  (225 shorter events, 156.5 us)
Async XLA Ops:
  0.6 1.2 copy-start
  1.8 0.7 copy-start.1
  3.4 18.8 %copy-start.4 = (f32[2,128,128]{2,1,0:T(8,128)S(1)}, f32[2,128,128]{2,1,0:T(8,128)}, u32[]{:S(2)}) copy-start(f32[2,128,128]{2,1,0:T(8,128)} %param.12) | copy-start | bytes 393220
  3.4 6.2 %collective-permute-start = (f32[32,896]{1,0:T(8,128)S(1)}, f32[32,896]{1,0:T(8,128)S(1)}, u32[]{:S(2)}, u32[]{:S(2)}) collective-permute-start(f32[32,896]{1,0:T(8,128)S(1)} %get-tuple-element.514), channel_id=1, source_target_pairs={{0,16},{16,0},{1,17},{17,1},{2,18},{18,2},{3,19},{19,3},{4,20},{20... | collective-permute-start | bytes 344072 | tf_op jit(solution)/shard_map/while/body/eval_jaxpr/ppermute | solution.py:20
  9.6 4.9 %collective-permute-start = (f32[32,896]{1,0:T(8,128)S(1)}, f32[32,896]{1,0:T(8,128)S(1)}, u32[]{:S(2)}, u32[]{:S(2)}) collective-permute-start(f32[32,896]{1,0:T(8,128)S(1)} %get-tuple-element.514), channel_id=1, source_target_pairs={{0,16},{16,0},{1,17},{17,1},{2,18},{18,2},{3,19},{19,3},{4,20},{20... | collective-permute-start | bytes 344072 | tf_op jit(solution)/shard_map/while/body/eval_jaxpr/ppermute | solution.py:20
  14.5 7.6 %copy-start.5 = (s32[2,1,1,14]{3,2,1,0:T(1,128)S(1)}, s32[2,1,1,14]{3,2,1,0:T(1,128)}, u32[]{:S(2)}) copy-start(s32[2,1,1,14]{3,2,1,0:T(1,128)} %param.14) | copy-start | bytes 340
  14.5 7.7 %collective-permute-start.1 = (f32[32,896]{1,0:T(8,128)S(1)}, f32[32,896]{1,0:T(8,128)S(1)}, u32[]{:S(2)}, u32[]{:S(2)}) collective-permute-start(f32[32,896]{1,0:T(8,128)S(1)} %get-tuple-element.260), channel_id=1, source_target_pairs={{0,2},{1,3},{2,4},{3,5},{4,6},{5,7},{6,8},{7,9},{8,10},{9,11},{10,... | collective-permute-start | bytes 344072 | tf_op jit(solution)/shard_map/ppermute | solution.py:26
  18.2 4.5 %collective-permute-start.2 = (f32[32,896]{1,0:T(8,128)S(1)}, f32[32,896]{1,0:T(8,128)S(1)}, u32[]{:S(2)}, u32[]{:S(2)}) collective-permute-start(f32[32,896]{1,0:T(8,128)S(1)} %get-tuple-element.260), channel_id=1, source_target_pairs={{0,1},{1,2},{2,3},{3,4},{4,5},{5,6},{6,7},{7,8},{8,9},{9,10},{10,1... | collective-permute-start | bytes 344072 | tf_op jit(solution)/shard_map/ppermute | solution.py:26
  19.5 5.0 %collective-permute-start.3 = (f32[32,896]{1,0:T(8,128)S(1)}, f32[32,896]{1,0:T(8,128)S(1)}, u32[]{:S(2)}, u32[]{:S(2)}) collective-permute-start(f32[32,896]{1,0:T(8,128)S(1)} %get-tuple-element.260), channel_id=1, source_target_pairs={{1,0},{2,1},{3,2},{4,3},{5,4},{6,5},{7,6},{8,7},{9,8},{10,9},{11,1... | collective-permute-start | bytes 344072 | tf_op jit(solution)/shard_map/ppermute | solution.py:26
  20.8 9.8 %collective-permute-start.4 = (f32[32,896]{1,0:T(8,128)S(1)}, f32[32,896]{1,0:T(8,128)S(1)}, u32[]{:S(2)}, u32[]{:S(2)}) collective-permute-start(f32[32,896]{1,0:T(8,128)S(1)} %get-tuple-element.260), channel_id=1, source_target_pairs={{2,0},{3,1},{4,2},{5,3},{6,4},{7,5},{8,6},{9,7},{10,8},{11,9},{12,... | collective-permute-start | bytes 344072 | tf_op jit(solution)/shard_map/ppermute | solution.py:26
  97.9 2.0 copy-start.3
  237.4 11.6 %collective-permute-start.10 = (f32[32,896]{1,0:T(8,128)S(1)}, f32[32,896]{1,0:T(8,128)S(1)}, u32[]{:S(2)}, u32[]{:S(2)}) collective-permute-start(f32[32,896]{1,0:T(8,128)S(1)} %get-tuple-element.350), channel_id=1, source_target_pairs={{1,0},{2,1},{3,2},{4,3},{5,4},{6,5},{7,6},{8,7},{9,8},{10,9},{11,1... | collective-permute-start | bytes 344072 | tf_op jit(solution)/shard_map/ppermute | solution.py:26
  238.7 13.7 %collective-permute-start.11 = (f32[32,896]{1,0:T(8,128)S(1)}, f32[32,896]{1,0:T(8,128)S(1)}, u32[]{:S(2)}, u32[]{:S(2)}) collective-permute-start(f32[32,896]{1,0:T(8,128)S(1)} %get-tuple-element.349), channel_id=1, source_target_pairs={{0,1},{1,2},{2,3},{3,4},{4,5},{5,6},{6,7},{7,8},{8,9},{9,10},{10,1... | collective-permute-start | bytes 344072 | tf_op jit(solution)/shard_map/ppermute | solution.py:26
  241.7 14.9 %collective-permute-start.12 = (f32[32,896]{1,0:T(8,128)S(1)}, f32[32,896]{1,0:T(8,128)S(1)}, u32[]{:S(2)}, u32[]{:S(2)}) collective-permute-start(f32[32,896]{1,0:T(8,128)S(1)} %get-tuple-element.348), channel_id=1, source_target_pairs={{0,2},{1,3},{2,4},{3,5},{4,6},{5,7},{6,8},{7,9},{8,10},{9,11},{10,... | collective-permute-start | bytes 344072 | tf_op jit(solution)/shard_map/ppermute | solution.py:26
  246.4 54.9 %collective-permute-start.5 = (f32[32,896]{1,0:T(8,128)S(1)}, f32[32,896]{1,0:T(8,128)S(1)}, u32[]{:S(2)}, u32[]{:S(2)}) collective-permute-start(f32[32,896]{1,0:T(8,128)S(1)} %get-tuple-element.343), channel_id=1, source_target_pairs={{2,0},{3,1},{4,2},{5,3},{6,4},{7,5},{8,6},{9,7},{10,8},{11,9},{12,... | collective-permute-start | bytes 344072 | tf_op jit(solution)/shard_map/ppermute | solution.py:26
  247.7 53.6 %collective-permute-start.6 = (f32[32,896]{1,0:T(8,128)S(1)}, f32[32,896]{1,0:T(8,128)S(1)}, u32[]{:S(2)}, u32[]{:S(2)}) collective-permute-start(f32[32,896]{1,0:T(8,128)S(1)} %get-tuple-element.346), channel_id=1, source_target_pairs={{1,0},{2,1},{3,2},{4,3},{5,4},{6,5},{7,6},{8,7},{9,8},{10,9},{11,1... | collective-permute-start | bytes 344072 | tf_op jit(solution)/shard_map/ppermute | solution.py:26
  249.0 52.3 %collective-permute-start.7 = (f32[32,896]{1,0:T(8,128)S(1)}, f32[32,896]{1,0:T(8,128)S(1)}, u32[]{:S(2)}, u32[]{:S(2)}) collective-permute-start(f32[32,896]{1,0:T(8,128)S(1)} %get-tuple-element.345), channel_id=1, source_target_pairs={{0,1},{1,2},{2,3},{3,4},{4,5},{5,6},{6,7},{7,8},{8,9},{9,10},{10,1... | collective-permute-start | bytes 344072 | tf_op jit(solution)/shard_map/ppermute | solution.py:26
  252.4 48.9 %collective-permute-start.8 = (f32[32,896]{1,0:T(8,128)S(1)}, f32[32,896]{1,0:T(8,128)S(1)}, u32[]{:S(2)}, u32[]{:S(2)}) collective-permute-start(f32[32,896]{1,0:T(8,128)S(1)} %get-tuple-element.344), channel_id=1, source_target_pairs={{0,2},{1,3},{2,4},{3,5},{4,6},{5,7},{6,8},{7,9},{8,10},{9,11},{10,... | collective-permute-start | bytes 344072 | tf_op jit(solution)/shard_map/ppermute | solution.py:26
  256.6 44.7 %collective-permute-start.9 = (f32[32,896]{1,0:T(8,128)S(1)}, f32[32,896]{1,0:T(8,128)S(1)}, u32[]{:S(2)}, u32[]{:S(2)}) collective-permute-start(f32[32,896]{1,0:T(8,128)S(1)} %get-tuple-element.347), channel_id=1, source_target_pairs={{2,0},{3,1},{4,2},{5,3},{6,4},{7,5},{8,6},{9,7},{10,8},{11,9},{12,... | collective-permute-start | bytes 344072 | tf_op jit(solution)/shard_map/ppermute | solution.py:26
  301.8 5.9 %copy-start.2 = (f32[1,2,32,896]{3,1,2,0:T(2,128)S(1)}, f32[1,2,32,896]{3,1,2,0:T(2,128)}, u32[]{:S(2)}) copy-start(f32[1,2,32,896]{3,1,2,0:T(2,128)} %copy-done.1) | copy-start | bytes 688132
  307.6 0.7 copy-start.6
where the time goes:
time: 317 us; the launch traced here: 311 us
  local copies, waits for them, and re-layouts  124 us (39%)
  loops' own time  52.6 us (17%)
  blocking collectives  49.2 us (16%)
  matrix products  35.2 us (11%)
  starting transfers between devices  32.7 us (10%)
  waiting for transfers between devices  11 us (3%)
  other arithmetic  4.47 us (1%)
    gather x84, local copies, waits for them, and re-layouts  54.7 us
    another operation x1, loops' own time, strip_update(): acc_real, acc_imag = lax.fori_loop(0, number, place, (zeros, zeros))  51.7 us
    psum x1, blocking collectives, body(): total_misfit = lax.psum(local_misfit, ('blk', 'wide'))  43.3 us
    ppermute x12, starting transfers between devices, from_behind(): return lax.ppermute(shard, axis, pairs)  27.8 us
    dynamic_update_slice x14, local copies, waits for them, and re-layouts, place(): lax.dynamic_update_slice(acc_imag, window(acc_imag, top, left) + corr_ima...  23.8 us
    dynamic_update_slice x14, local copies, waits for them, and re-layouts, place(): lax.dynamic_update_slice(acc_real, window(acc_real, top, left) + corr_rea...  23.8 us
    dot_general x8, matrix products, left_apply(): return jnp.einsum('jk,bkl->bjl', table, batch, precision=highest)  15.7 us
    dot_general x8, matrix products, right_apply(): return jnp.einsum('bjk,kl->bjl', batch, table, precision=highest)  15.5 us
  transfers between devices with their start and end apart: 14, of which 4 were waited for; matrix products, arithmetic and copies ran while one was open for 1% of the time, Pallas kernels for 0%

commit v1 on v0

v1 whole, which is shorter than its diff:
```python
import functools
import math

import jax
import jax.numpy as jnp
import numpy as np
from jax import lax
from jax.experimental import pallas as pl
from jax.experimental.pallas import tpu as pltpu
from jax.sharding import PartitionSpec as P

PATCH = 128
LANES = 128
MESH = pl.DeviceIdType.MESH
F32 = jnp.float32
BF16 = jnp.bfloat16
floor_value = 0.25

PHASE_MOVES = ((2, 8, 32, 0), (1, 0, 32, 24), (-1, 0, 32, 88), (-2, 0, 24, 120))
GRAD_MOVES = ((2, 120, 144, 0), (1, 88, 120, 0), (-1, 24, 56, 0), (-2, 0, 24, 8))
OWN_FIRST = 56
STRIP = 144


def dft_tables(length):
    grid = np.arange(length)
    angles = (grid[:, None] * grid[None, :] % length) * (2.0 * math.pi / length)
    cos = np.cos(angles) / math.sqrt(length)
    sin = -np.sin(angles) / math.sqrt(length)
    left = np.block([[cos, -sin], [sin, cos]])
    tables = []
    for whole in (left, left.T):
        high = whole.astype(jnp.bfloat16)
        low = (whole - high.astype(np.float64)).astype(jnp.bfloat16)
        tables += [high, low]
    return tables


def sin_cos(x):
    turns = jnp.floor(x * (2.0 / math.pi) + (0.5))
    r = x - turns * (1.5703125)
    r = r - turns * (4.837512969970703125e-4)
    r = r - turns * (7.54978995489188216e-8)
    z = r * r
    s = (((-1.9515295891e-4) * z + (8.3321608736e-3)) * z + (-1.6666654611e-1)) * z * r + r
    c = (((2.443315711809948e-5) * z + (-1.388731625493765e-3)) * z + (4.166664568298827e-2)) * z * z
    c = c - (0.5) * z + (1.0)
    quad = turns.astype(jnp.int32)
    odd = (quad & 1) == 1
    sin_out = jnp.where(odd, c, s)
    cos_out = jnp.where(odd, s, c)
    sin_out = jnp.where((quad & 2) == 2, -sin_out, sin_out)
    cos_out = jnp.where(((quad + 1) & 2) == 2, -cos_out, cos_out)
    return sin_out, cos_out


def split(x):
    high = x.astype(BF16)
    return high, (x - high.astype(F32)).astype(BF16)


def dot(a, b):
    return jnp.dot(a, b, preferred_element_type=F32)


def from_left(high, low, x):
    xh, xl = split(x)
    return dot(jnp.concatenate([high, high, low], 1), jnp.concatenate([xh, xl, xh], 0))


def from_right(x, high, low):
    xh, xl = split(x)
    return dot(jnp.concatenate([xh, xl, xh], 1), jnp.concatenate([high, high, low], 0))


def kernel(
    groups, columns, near,
    path_ref, jit_ref, slab_ref, probe_ref, meas_ref, th_ref, tl_ref, rh_ref, rl_ref,
    grad_out, mis_out,
    asend, arecv, ph, objr, obji, gacc, cbuf, gbuf, mis1, mis2,
    a_s, a_r, b_s, b_r, c_s, c_r, d_s, d_r, m1_s, m1_r, m2_s, m2_r,
):
    group = lax.axis_index("blk")
    me = lax.axis_index("wide")
    layers, rows, cols = slab_ref.shape
    tiles = cols // LANES
    far_count = columns // near
    my_near = lax.rem(me, near)
    my_far = me // near
    first_near = me - my_near
    near_all = groups * near
    near_id = group * near + my_near

    def near_device(step):
        other = lax.rem(near_id + step, near_all)
        return (other // near, first_near + lax.rem(other, near))

    def far_device(step):
        return (group, lax.rem(my_far + step, far_count) * near + my_near)

    def there(offset):
        return (me + offset >= 0) & (me + offset < columns)

    barrier = pltpu.get_barrier_semaphore()
    for step in range(1, near_all):
        pl.semaphore_signal(barrier, inc=1, device_id=near_device(step), device_id_type=MESH)
    for step in range(1, far_count):
        pl.semaphore_signal(barrier, inc=1, device_id=far_device(step), device_id_type=MESH)
    for offset, *_ in PHASE_MOVES:
        @pl.when(there(offset))
        def _():
            pl.semaphore_signal(barrier, inc=1, device_id=(group, me + offset), device_id_type=MESH)

    def slab_term(angle, tile):
        total = path_ref[angle, group, 0] * slab_ref[0, :, tile * LANES : (tile + 1) * LANES]
        for layer in range(1, layers):
            total = total + path_ref[angle, group, layer] * slab_ref[layer, :, tile * LANES : (tile + 1) * LANES]
        return total

    for tile in range(tiles):
        for step in range(1, groups):
            asend[step - 1, tile] = slab_term(lax.rem(group + step, groups), tile)
        ph[tile, OWN_FIRST : OWN_FIRST + rows] = slab_term(group, tile)
    zero = jnp.zeros((STRIP, LANES), F32)
    for edge in (0, tiles + 1):
        objr[edge] = zero
        obji[edge] = zero
    gacc[0] = zero
    gacc[1] = zero

    partners = near_all - 1 + far_count - 1
    for offset, *_ in PHASE_MOVES:
        partners = partners + there(offset).astype(jnp.int32)
    pl.semaphore_wait(barrier, partners)

    def remote(src, dst, send, recv, device):
        return pltpu.make_async_remote_copy(
            src_ref=src, dst_ref=dst, send_sem=send, recv_sem=recv, device_id=device, device_id_type=MESH
        )

    def angle_copy(step, tile):
        device = (lax.rem(group + step, groups), me)
        return remote(asend.at[step - 1, tile], arecv.at[step - 1, tile], a_s.at[step - 1, tile], a_r.at[step - 1, tile], device)

    def phase_copy(way, tile):
        offset, lo, hi, at = PHASE_MOVES[way]
        return remote(
            ph.at[tile, pl.ds(OWN_FIRST + lo, hi - lo)], ph.at[tile, pl.ds(at, hi - lo)],
            b_s.at[way, tile], b_r.at[way, tile], (group, me + offset),
        )

    def grad_copy(way, tile):
        offset, lo, hi, at = GRAD_MOVES[way]
        return remote(
            gacc.at[tile + 1, pl.ds(lo, hi - lo)], cbuf.at[way, tile, pl.ds(at, hi - lo)],
            c_s.at[way, tile], c_r.at[way, tile], (group, me + offset),
        )

    def share_copy(step, tile):
        device = (lax.rem(group + step, groups), me)
        return remote(gbuf.at[0, tile], gbuf.at[step, tile], d_s.at[step - 1, tile], d_r.at[step - 1, tile], device)

    def ways(fn, sign):
        for way, (offset, *_) in enumerate(PHASE_MOVES):
            @pl.when(there(sign * offset))
            def _():
                fn(way)

    for tile in range(tiles):
        for step in range(1, groups):
            angle_copy(step, tile).start()

    def spread(tile, carry):
        own = ph[tile, OWN_FIRST : OWN_FIRST + rows]
        for step in range(1, groups):
            angle_copy(step, tile).wait_recv()
            own = own + arecv[step - 1, tile]
        ph[tile, OWN_FIRST : OWN_FIRST + rows] = own
        ways(lambda way: phase_copy(way, tile).start(), 1)
        return carry

    lax.fori_loop(0, tiles, spread, 0)

    row_iota = lax.broadcasted_iota(jnp.int32, (STRIP, LANES), 0)
    grid_row = row_iota + (me * rows - OWN_FIRST)
    inside = (grid_row >= 0) & (grid_row < rows * columns)

    def prepare(tile):
        ways(lambda way: phase_copy(way, tile).wait_recv(), -1)
        s, c = sin_cos(ph[tile])
        objr[tile + 1] = jnp.where(inside, c, 0.0)
        obji[tile + 1] = jnp.where(inside, s, 0.0)

    def finish(tile):
        ways(lambda way: grad_copy(way, tile).wait_recv(), -1)
        total = gacc[tile + 1, OWN_FIRST : OWN_FIRST + rows]
        row = lax.broadcasted_iota(jnp.int32, (rows, LANES), 0)
        for way, (offset, lo, hi, at) in enumerate(GRAD_MOVES):
            ok = (row >= at) & (row < at + hi - lo) & there(-offset)
            total = total + jnp.where(ok, cbuf[way, tile], 0.0)
        gbuf[0, tile] = total
        for step in range(1, groups):
            share_copy(step, tile).start()

    lane = lax.broadcasted_iota(jnp.int32, (STRIP, LANES), 1)
    row16 = lax.broadcasted_iota(jnp.int32, (STRIP - PATCH, LANES), 0)
    extra = STRIP - PATCH

    def pair(p, misfit):
        @pl.when(p + 1 < tiles)
        def _():
            prepare(p + 1)

        waves, objects, probes, shifts = [], [], [], []
        for half in range(2):
            position = 2 * p + half
            jr = jit_ref[0, position]
            start = jit_ref[1, position] + (PATCH - 40 if half == 0 else PATCH // 2 - 40)
            keep = lane >= start

            def wrapped(image):
                tall = jnp.where(keep, image[p + half], image[p + half + 1])
                top = jnp.where(row16 >= jr, tall[:extra], tall[PATCH:])
                return jnp.concatenate([top, tall[extra:PATCH]], 0)

            o_r, o_i = wrapped(objr), wrapped(obji)
            p_r = pltpu.roll(pltpu.roll(probe_ref[0], jr, 0), start, 1)
            p_i = pltpu.roll(pltpu.roll(probe_ref[1], jr, 0), start, 1)
            waves.append(jnp.concatenate([p_r * o_r - p_i * o_i, p_r * o_i + p_i * o_r], 0))
            objects.append((o_r, o_i))
            probes.append((p_r, p_i))
            shifts.append((jr, keep))
        th, tl, rh, rl = th_ref[...], tl_ref[...], rh_ref[...], rl_ref[...]
        wave = jnp.concatenate(waves, 1)

        def restack(x):
            upper = jnp.concatenate([x[:PATCH, :PATCH], x[PATCH:, :PATCH]], 1)
            lower = jnp.concatenate([x[:PATCH, PATCH:], x[PATCH:, PATCH:]], 1)
            return jnp.concatenate([upper, lower], 0)

        far = from_right(restack(from_left(th, tl, wave)), rh, rl)
        f_r, f_i = far[:, :PATCH], far[:, PATCH:]
        square = f_r * f_r + f_i * f_i
        inverse = lax.rsqrt(jnp.maximum(square, (1e-35)))
        target = meas_ref[pl.ds(2 * p, 2)].reshape(2 * PATCH, PATCH).astype(F32)
        error = square * inverse - target
        misfit = misfit + jnp.sum((error * error).reshape(2 * PATCH // 8, 8, PATCH), axis=0)
        ratio = target * jnp.minimum(inverse, (1.0 / floor_value))
        level = jnp.concatenate([ratio * f_r, ratio * f_i], 1)
        back = from_left(rh, rl, restack(from_right(level, th, tl)))
        diff = back - wave
        parts = []
        for half in range(2):
            d = diff[:, half * PATCH : (half + 1) * PATCH]
            d_r, d_i = d[:PATCH], d[PATCH:]
            (p_r, p_i), (o_r, o_i), (jr, keep) = probes[half], objects[half], shifts[half]
            c_re = p_r * d_r + p_i * d_i
            c_im = p_r * d_i - p_i * d_r
            g = o_r * c_im - o_i * c_re
            below = row16 >= jr
            tall = jnp.concatenate(
                [jnp.where(below, g[:extra], 0.0), g[extra:], jnp.where(below, 0.0, g[:extra])], 0
            )
            parts.append((jnp.where(keep, tall, 0.0), jnp.where(keep, 0.0, tall)))
        gacc[p] = gacc[p] + parts[0][0]
        gacc[p + 1] = gacc[p + 1] + (parts[0][1] + parts[1][0])
        gacc[p + 2] = parts[1][1]

        @pl.when(p >= 1)
        def _():
            ways(lambda way: grad_copy(way, p - 1).start(), 1)

        @pl.when(p >= 3)
        def _():
            finish(p - 3)

        return misfit

    prepare(0)
    misfit = lax.fori_loop(0, tiles, pair, jnp.zeros((8, PATCH), F32))
    ways(lambda way: grad_copy(way, tiles - 1).start(), 1)

    mis1[near_id] = misfit

    def near_copy(step):
        return remote(mis1.at[near_id], mis1.at[near_id], m1_s.at[step - 1], m1_r.at[step - 1], near_device(step))

    def far_copy(step):
        return remote(mis2.at[my_far], mis2.at[my_far], m2_s.at[step - 1], m2_r.at[step - 1], far_device(step))

    for step in range(1, near_all):
        near_copy(step).start()
    finish(tiles - 3)
    for step in range(1, near_all):
        near_copy(step).wait_recv()
    mis2[my_far] = jnp.sum(mis1[...], axis=0)
    for step in range(1, far_count):
        far_copy(step).start()
    finish(tiles - 2)
    finish(tiles - 1)

    def collect(tile, carry):
        for step in range(1, groups):
            share_copy(step, tile).wait_recv()
            angle_copy(step, tile).wait_send()
            share_copy(step, tile).wait_send()
        ways(lambda way: phase_copy(way, tile).wait_send(), 1)
        ways(lambda way: grad_copy(way, tile).wait_send(), 1)
        return carry

    lax.fori_loop(0, tiles, collect, 0)
    for tile in range(tiles):
        for step in range(groups):
            angle = lax.rem(group - step + groups, groups)
            grad_out[angle, :, tile * LANES : (tile + 1) * LANES] = gbuf[step, tile]
    for step in range(1, near_all):
        near_copy(step).wait_send()
    for step in range(1, far_count):
        far_copy(step).wait_recv()
    total = jnp.sum(mis2[...], axis=0)
    mis_out[...] = jnp.sum(total, keepdims=True)
    for step in range(1, far_count):
        far_copy(step).wait_send()


def body(mesh, volume, path_lengths, probe, measured, jitter, step_sizes):
    groups, columns = mesh.shape["blk"], mesh.shape["wide"]
    near = math.gcd(columns, 4)
    slab = volume[0]
    layers, rows, cols = slab.shape
    tiles = cols // LANES
    tables = [jnp.asarray(t) for t in dft_tables(probe.shape[-1])]
    vmem = pl.BlockSpec(memory_space=pltpu.VMEM)
    smem = pl.BlockSpec(memory_space=pltpu.SMEM)
    sem = pltpu.SemaphoreType.DMA
    others = max(groups - 1, 1)
    grads, misfit = pl.pallas_call(
        functools.partial(kernel, groups, columns, near),
        out_shape=(
            jax.ShapeDtypeStruct((groups, rows, cols), F32),
            jax.ShapeDtypeStruct((1, 1), F32),
        ),
        in_specs=[smem, smem] + [vmem] * 7,
        out_specs=(vmem, vmem),
        scratch_shapes=[
            pltpu.VMEM((others, tiles, rows, LANES), F32),
            pltpu.VMEM((others, tiles, rows, LANES), F32),
            pltpu.VMEM((tiles, STRIP, LANES), F32),
            pltpu.VMEM((tiles + 2, STRIP, LANES), F32),
            pltpu.VMEM((tiles + 2, STRIP, LANES), F32),
            pltpu.VMEM((tiles + 2, STRIP, LANES), F32),
            pltpu.VMEM((4, tiles, rows, LANES), F32),
            pltpu.VMEM((groups, tiles, rows, LANES), F32),
            pltpu.VMEM((groups * near, 8, LANES), F32),
            pltpu.VMEM((columns // near, 8, LANES), F32),
            sem((others, tiles)), sem((others, tiles)),
            sem((4, tiles)), sem((4, tiles)),
            sem((4, tiles)), sem((4, tiles)),
            sem((others, tiles)), sem((others, tiles)),
            sem((groups * near,)), sem((groups * near,)),
            sem((columns // near,)), sem((columns // near,)),
        ],
        compiler_params=pltpu.CompilerParams(collective_id=0, has_side_effects=True),
    )(path_lengths, jitter[:, 0, 0], slab, probe, measured[0, 0], *tables)
    group = lax.axis_index("blk")
    own_paths = lax.dynamic_index_in_dim(path_lengths, group, 1, keepdims=False)
    coeffs = step_sizes[:, None] * own_paths
    update = coeffs[0][:, None, None] * grads[0]
    for angle in range(1, groups):
        update = update + coeffs[angle][:, None, None] * grads[angle]
    return ((slab - update)[None], misfit[0, 0])


def solution(mesh):
    in_specs = (
        P("blk", None, "wide", None),
        P(),
        P(),
        P("blk", "wide", None, None, None),
        P(None, "blk", "wide", None),
        P(),
    )
    out_specs = (P("blk", None, "wide", None), P())
    return jax.shard_map(
        functools.partial(body, mesh), mesh=mesh, in_specs=in_specs, out_specs=out_specs, check_vma=False
    )
```

time: 317 us -> 41.5 us (0.13); the launches traced: 311 us -> 41.3 us
  local copies, waits for them, and re-layouts: 124 us -> 2.38 us
  loops' own time: 52.6 us -> 0 us
  blocking collectives: 49.2 us -> 0 us
  Pallas kernels: 0 us -> 35.6 us
  matrix products: 35.2 us -> 0 us
  starting transfers between devices: 32.7 us -> 0 us
  waiting for transfers between devices: 11 us -> 0 us
  other arithmetic: 4.47 us -> 0.86 us
    gather x84 -> x0, local copies, waits for them, and re-layouts: 54.7 us -> none
    another operation x4 -> x0, loops' own time: 52.6 us -> none  [the longest x1 51.7 us: strip_update(): acc_real, acc_imag = lax.fori_loop(0, number, place, (zeros, zeros))]
    dynamic_update_slice x28 -> x0, local copies, waits for them, and re-layouts: 47.7 us -> none  [the longest x14 23.8 us: place(): lax.dynamic_update_slice(acc_imag, window(acc_imag, top, left) + corr_ima...]
    psum x1 -> x0, blocking collectives: 43.3 us -> none  [body(): total_misfit = lax.psum(local_misfit, ('blk', 'wide'))]
    pallas_call x0 -> x1, Pallas kernels: none -> 35.6 us  [body(): pl.pallas_call(functools.partial(kernel, groups, columns, near), out_shap...]
    dot_general x20 -> x0, matrix products: 35.2 us -> none  [the longest x8 15.7 us: left_apply(): return jnp.einsum('jk,bkl->bjl', table, batch, precision=highest)]
    ppermute x14 -> x0, starting transfers between devices: 32.7 us -> none  [the longest x12 27.8 us: from_behind(): return lax.ppermute(shard, axis, pairs)]
    dynamic_slice x28 -> x0, local copies, waits for them, and re-layouts: 17.4 us -> none  [the longest x14 8.68 us: place(): left = starts_col[position]]
  transfers between devices with their start and end apart: 14 -> 0, of which waited for: 4 -> 0; matrix products, arithmetic and copies ran while one was open for 1% -> 0% of each run, Pallas kernels for 0% -> 0%
where the time goes in v1:
time: 41.5 us; the launch traced here: 41.3 us
  Pallas kernels  35.6 us (86%)
  between operations  2.48 us (6%)
  local copies, waits for them, and re-layouts  2.38 us (6%)
  other arithmetic  0.86 us (2%)
    pallas_call x1, Pallas kernels, body(): pl.pallas_call(functools.partial(kernel, groups, columns, near), out_shap...  35.6 us
    unnamed x6, local copies, waits for them, and re-layouts  1.36 us
    mul x2, local copies, waits for them, and re-layouts, body(): update = coeffs[0][:, None, None] * grads[0]  1.02 us

profile of v1, /device:TPU:0, one launch (start us, length us, event | category | flops | bytes accessed | tf_op | source)
XLA Modules:
  0.0 41.3 jit_solution(12677583859625368743)
XLA Ops:
  0.6 0.0 copy-start.1
  0.6 0.7 %copy-done.1 = f32[2,2,2]{2,1,0:T(2,128)S(1)} copy-done((f32[2,2,2]{2,1,0:T(2,128)S(1)}, f32[2,2,2]{2,1,0:T(2,128)}, u32[]{:S(2)}) %copy-start.1) | copy-done | bytes 56
  1.3 0.0 copy-start.2
  1.3 0.7 %copy-done.2 = f32[2]{0:T(128)S(1)} copy-done((f32[2]{0:T(128)S(1)}, f32[2]{0:T(128)}, u32[]{:S(2)}) %copy-start.2) | copy-done | bytes 32
  2.0 0.1 broadcast_multiply_fusion
  2.1 35.6 %shard_map.113 = (f32[2,32,896]{2,1,0:T(8,128)}, f32[1,1]{1,0:T(1,128)}) custom-call(f32[2,2,2]{2,1,0:T(2,128)} %path_ref.1, s32[2,14]{1,0:T(2,128)} %bitcast.16, f32[2,32,896]{2,1,0:T(8,128)} %bitcast.13, f32[2,128,128]{2,1,0:T(8,128)} %probe_ref.1, bf16[14,128,128]{2,1,0:T(8,128)(2,1)} %bitcast.14, bf16[256,256]{1,0:T(8,128)(2,1)} %constant.20.clone.th_ref, ...), custom_call_target="tpu_custom_call" | custom-call | tf_op jit(solution)/shard_map/pallas_call | solution.py:337
  37.6 0.0 copy-start
  37.7 1.0 %slice_bitcast_fusion.1 = (f32[32,896]{1,0:T(8,128)S(1)}, f32[32,896]{1,0:T(8,128)S(1)}) fusion(f32[2,32,896]{2,1,0:T(8,128)} %get-tuple-element.4), kind=kLoop, calls=%fused_computation.2 | loop fusion | bytes 458752 | tf_op jit(solution)/shard_map/mul | solution.py:368
  38.7 0.0 copy-done
  38.7 0.8 %add_subtract_fusion = f32[1,2,32,896]{3,2,1,0:T(8,128)} fusion(f32[1,2,32,896]{3,2,1,0:T(8,128)S(1)} %copy-done, f32[32,896]{1,0:T(8,128)S(1)} %get-tuple-element.7, f32[2]{0:T(128)S(1)} %get-tuple-element.9, f32[32,896]{1,0:T(8,128)S(1)} %get-tuple-element.6, f32[2]{0:T(128)S(1)} %get-tuple-element.8), kind=kLoop, calls=%fused_computation | loop fusion | flops 229376 | bytes 688144 | tf_op jit(solution)/shard_map/sub | solution.py:371
  (2 shorter events, 0.0 us)
Async XLA Ops:
  0.6 0.7 %copy-start.1 = (f32[2,2,2]{2,1,0:T(2,128)S(1)}, f32[2,2,2]{2,1,0:T(2,128)}, u32[]{:S(2)}) copy-start(f32[2,2,2]{2,1,0:T(2,128)} %path_ref.1) | copy-start | bytes 100
  1.3 0.7 %copy-start.2 = (f32[2]{0:T(128)S(1)}, f32[2]{0:T(128)}, u32[]{:S(2)}) copy-start(f32[2]{0:T(128)} %param.15) | copy-start | bytes 28
  37.6 1.1 %copy-start = (f32[1,2,32,896]{3,2,1,0:T(8,128)S(1)}, f32[1,2,32,896]{3,2,1,0:T(8,128)}, u32[]{:S(2)}) copy-start(f32[1,2,32,896]{3,2,1,0:T(8,128)} %param.10) | copy-start | bytes 688132

commit v2 on v1

--- a/solution.py
+++ b/solution.py
@@ -75,9 +75,10 @@
 
 def kernel(
     groups, columns, near,
-    path_ref, jit_ref, slab_ref, probe_ref, meas_ref, th_ref, tl_ref, rh_ref, rl_ref,
-    grad_out, mis_out,
-    asend, arecv, ph, objr, obji, gacc, cbuf, gbuf, mis1, mis2,
+    path_ref, jit_ref, step_ref, slab_hbm, probe_hbm, meas_hbm, th_hbm, tl_hbm, rh_hbm, rl_hbm,
+    new_out, mis_out,
+    slab_ref, probe_ref, meas_ref, th_ref, tl_ref, rh_ref, rl_ref, in_sem,
+    wave_ref, level_ref, own_ref, asend, arecv, ph, objr, obji, gacc, cbuf, gbuf, mis1, mis2,
     a_s, a_r, b_s, b_r, c_s, c_r, d_s, d_r, m1_s, m1_r, m2_s, m2_r,
 ):
     group = lax.axis_index("blk")
@@ -101,6 +102,14 @@
     def there(offset):
         return (me + offset >= 0) & (me + offset < columns)
 
+    loads = [
+        pltpu.make_async_copy(src, dst, in_sem.at[i])
+        for i, (src, dst) in enumerate((
+            (slab_hbm, slab_ref), (probe_hbm, probe_ref), (meas_hbm, meas_ref),
+            (th_hbm, th_ref), (tl_hbm, tl_ref), (rh_hbm, rh_ref), (rl_hbm, rl_ref),
+        ))
+    ]
+    loads[0].start()
     barrier = pltpu.get_barrier_semaphore()
     for step in range(1, near_all):
         pl.semaphore_signal(barrier, inc=1, device_id=near_device(step), device_id_type=MESH)
@@ -117,6 +126,9 @@
             total = total + path_ref[angle, group, layer] * slab_ref[layer, :, tile * LANES : (tile + 1) * LANES]
         return total
 
+    for load in loads[1:]:
+        load.start()
+    loads[0].wait()
     for tile in range(tiles):
         for step in range(1, groups):
             asend[step - 1, tile] = slab_term(lax.rem(group + step, groups), tile)
@@ -206,16 +218,20 @@
     row16 = lax.broadcasted_iota(jnp.int32, (STRIP - PATCH, LANES), 0)
     extra = STRIP - PATCH
 
-    def pair(p, misfit):
-        @pl.when(p + 1 < tiles)
-        def _():
-            prepare(p + 1)
-
-        waves, objects, probes, shifts = [], [], [], []
+    def restack(x):
+        upper = jnp.concatenate([x[:PATCH, :PATCH], x[PATCH:, :PATCH]], 1)
+        lower = jnp.concatenate([x[:PATCH, PATCH:], x[PATCH:, PATCH:]], 1)
+        return jnp.concatenate([upper, lower], 0)
+
+    def shift_of(p, half):
+        position = 2 * p + half
+        return jit_ref[0, position], jit_ref[1, position] + (PATCH - 40 if half == 0 else PATCH // 2 - 40)
+
+    def forward(p):
+        slot = p % 2
+        waves = []
         for half in range(2):
-            position = 2 * p + half
-            jr = jit_ref[0, position]
-            start = jit_ref[1, position] + (PATCH - 40 if half == 0 else PATCH // 2 - 40)
+            jr, start = shift_of(p, half)
             keep = lane >= start
 
             def wrapped(image):
@@ -227,33 +243,31 @@
             p_r = pltpu.roll(pltpu.roll(probe_ref[0], jr, 0), start, 1)
             p_i = pltpu.roll(pltpu.roll(probe_ref[1], jr, 0), start, 1)
             waves.append(jnp.concatenate([p_r * o_r - p_i * o_i, p_r * o_i + p_i * o_r], 0))
-            objects.append((o_r, o_i))
-            probes.append((p_r, p_i))
-            shifts.append((jr, keep))
-        th, tl, rh, rl = th_ref[...], tl_ref[...], rh_ref[...], rl_ref[...]
+            for index, value in enumerate((o_r, o_i, p_r, p_i)):
+                own_ref[slot, half, index] = value
         wave = jnp.concatenate(waves, 1)
-
-        def restack(x):
-            upper = jnp.concatenate([x[:PATCH, :PATCH], x[PATCH:, :PATCH]], 1)
-            lower = jnp.concatenate([x[:PATCH, PATCH:], x[PATCH:, PATCH:]], 1)
-            return jnp.concatenate([upper, lower], 0)
-
-        far = from_right(restack(from_left(th, tl, wave)), rh, rl)
+        wave_ref[slot] = wave
+        far = from_right(restack(from_left(th_ref[...], tl_ref[...], wave)), rh_ref[...], rl_ref[...])
         f_r, f_i = far[:, :PATCH], far[:, PATCH:]
         square = f_r * f_r + f_i * f_i
         inverse = lax.rsqrt(jnp.maximum(square, (1e-35)))
-        target = meas_ref[pl.ds(2 * p, 2)].reshape(2 * PATCH, PATCH).astype(F32)
+        target = meas_ref[2 * p : 2 * p + 2].reshape(2 * PATCH, PATCH).astype(F32)
         error = square * inverse - target
-        misfit = misfit + jnp.sum((error * error).reshape(2 * PATCH // 8, 8, PATCH), axis=0)
         ratio = target * jnp.minimum(inverse, (1.0 / floor_value))
-        level = jnp.concatenate([ratio * f_r, ratio * f_i], 1)
-        back = from_left(rh, rl, restack(from_right(level, th, tl)))
-        diff = back - wave
+        level_ref[slot] = jnp.concatenate([ratio * f_r, ratio * f_i], 1)
+        return jnp.sum((error * error).reshape(2 * PATCH // 8, 8, PATCH), axis=0)
+
+    def backward(p):
+        slot = p % 2
+        back = from_left(rh_ref[...], rl_ref[...], restack(from_right(level_ref[slot], th_ref[...], tl_ref[...])))
+        diff = back - wave_ref[slot]
         parts = []
         for half in range(2):
+            jr, start = shift_of(p, half)
+            keep = lane >= start
             d = diff[:, half * PATCH : (half + 1) * PATCH]
             d_r, d_i = d[:PATCH], d[PATCH:]
-            (p_r, p_i), (o_r, o_i), (jr, keep) = probes[half], objects[half], shifts[half]
+            o_r, o_i, p_r, p_i = (own_ref[slot, half, index] for index in range(4))
             c_re = p_r * d_r + p_i * d_i
             c_im = p_r * d_i - p_i * d_r
             g = o_r * c_im - o_i * c_re
@@ -266,53 +280,60 @@
         gacc[p + 1] = gacc[p + 1] + (parts[0][1] + parts[1][0])
         gacc[p + 2] = parts[1][1]
 
-        @pl.when(p >= 1)
-        def _():
-            ways(lambda way: grad_copy(way, p - 1).start(), 1)
-
-        @pl.when(p >= 3)
-        def _():
-            finish(p - 3)
-
-        return misfit
-
-    prepare(0)
-    misfit = lax.fori_loop(0, tiles, pair, jnp.zeros((8, PATCH), F32))
-    ways(lambda way: grad_copy(way, tiles - 1).start(), 1)
-
-    mis1[near_id] = misfit
-
     def near_copy(step):
         return remote(mis1.at[near_id], mis1.at[near_id], m1_s.at[step - 1], m1_r.at[step - 1], near_device(step))
 
     def far_copy(step):
         return remote(mis2.at[my_far], mis2.at[my_far], m2_s.at[step - 1], m2_r.at[step - 1], far_device(step))
 
-    for step in range(1, near_all):
-        near_copy(step).start()
-    finish(tiles - 3)
+    prepare(0)
+    prepare(1)
+    for load in loads[1:]:
+        load.wait()
+    misfit = forward(0)
+    for p in range(tiles):
+        if p + 2 < tiles:
+            prepare(p + 2)
+        backward(p)
+        if p + 1 < tiles:
+            misfit = misfit + forward(p + 1)
+        if p >= 1:
+            ways(lambda way: grad_copy(way, p - 1).start(), 1)
+        if p == tiles - 2:
+            mis1[near_id] = jnp.sum(misfit, axis=0, keepdims=True)
+            for step in range(1, near_all):
+                near_copy(step).start()
+        if p >= 3:
+            finish(p - 3)
+    ways(lambda way: grad_copy(way, tiles - 1).start(), 1)
     for step in range(1, near_all):
         near_copy(step).wait_recv()
     mis2[my_far] = jnp.sum(mis1[...], axis=0)
     for step in range(1, far_count):
         far_copy(step).start()
+    finish(tiles - 3)
     finish(tiles - 2)
     finish(tiles - 1)
 
     def collect(tile, carry):
         for step in range(1, groups):
-            share_copy(step, tile).wait_recv()
             angle_copy(step, tile).wait_send()
             share_copy(step, tile).wait_send()
         ways(lambda way: phase_copy(way, tile).wait_send(), 1)
         ways(lambda way: grad_copy(way, tile).wait_send(), 1)
         return carry
 
-    lax.fori_loop(0, tiles, collect, 0)
     for tile in range(tiles):
+        span = slice(tile * LANES, (tile + 1) * LANES)
+        news = [jnp.zeros((rows, LANES), F32)] * layers
         for step in range(groups):
+            if step > 0:
+                share_copy(step, tile).wait_recv()
             angle = lax.rem(group - step + groups, groups)
-            grad_out[angle, :, tile * LANES : (tile + 1) * LANES] = gbuf[step, tile]
+            for layer in range(layers):
+                news[layer] = news[layer] + (step_ref[angle] * path_ref[angle, group, layer]) * gbuf[step, tile]
+        for layer in range(layers):
+            new_out[0, layer, :, span] = news[layer]
     for step in range(1, near_all):
         near_copy(step).wait_send()
     for step in range(1, far_count):
@@ -321,6 +342,7 @@
     mis_out[...] = jnp.sum(total, keepdims=True)
     for step in range(1, far_count):
         far_copy(step).wait_send()
+    lax.fori_loop(0, tiles, collect, 0)
 
 
 def body(mesh, volume, path_lengths, probe, measured, jitter, step_sizes):
@@ -332,17 +354,24 @@
     tables = [jnp.asarray(t) for t in dft_tables(probe.shape[-1])]
     vmem = pl.BlockSpec(memory_space=pltpu.VMEM)
     smem = pl.BlockSpec(memory_space=pltpu.SMEM)
+    hbm = pl.BlockSpec(memory_space=pl.ANY)
     sem = pltpu.SemaphoreType.DMA
+    loaded = [slab, probe, measured[0, 0], *tables]
     others = max(groups - 1, 1)
-    grads, misfit = pl.pallas_call(
+    new, misfit = pl.pallas_call(
         functools.partial(kernel, groups, columns, near),
         out_shape=(
-            jax.ShapeDtypeStruct((groups, rows, cols), F32),
+            jax.ShapeDtypeStruct((1, layers, rows, cols), F32),
             jax.ShapeDtypeStruct((1, 1), F32),
         ),
-        in_specs=[smem, smem] + [vmem] * 7,
+        in_specs=[smem] * 3 + [hbm] * 7,
         out_specs=(vmem, vmem),
         scratch_shapes=[
+            *(pltpu.VMEM(x.shape, x.dtype) for x in loaded),
+            sem((len(loaded),)),
+            pltpu.VMEM((2, 2 * PATCH, 2 * PATCH), F32),
+            pltpu.VMEM((2, 2 * PATCH, 2 * PATCH), F32),
+            pltpu.VMEM((2, 2, 4, PATCH, PATCH), F32),
             pltpu.VMEM((others, tiles, rows, LANES), F32),
             pltpu.VMEM((others, tiles, rows, LANES), F32),
             pltpu.VMEM((tiles, STRIP, LANES), F32),
@@ -351,8 +380,8 @@
             pltpu.VMEM((tiles + 2, STRIP, LANES), F32),
             pltpu.VMEM((4, tiles, rows, LANES), F32),
             pltpu.VMEM((groups, tiles, rows, LANES), F32),
-            pltpu.VMEM((groups * near, 8, LANES), F32),
-            pltpu.VMEM((columns // near, 8, LANES), F32),
+            pltpu.VMEM((groups * near, 1, LANES), F32),
+            pltpu.VMEM((columns // near, 1, LANES), F32),
             sem((others, tiles)), sem((others, tiles)),
             sem((4, tiles)), sem((4, tiles)),
             sem((4, tiles)), sem((4, tiles)),
@@ -361,14 +390,8 @@
             sem((columns // near,)), sem((columns // near,)),
         ],
         compiler_params=pltpu.CompilerParams(collective_id=0, has_side_effects=True),
-    )(path_lengths, jitter[:, 0, 0], slab, probe, measured[0, 0], *tables)
-    group = lax.axis_index("blk")
-    own_paths = lax.dynamic_index_in_dim(path_lengths, group, 1, keepdims=False)
-    coeffs = step_sizes[:, None] * own_paths
-    update = coeffs[0][:, None, None] * grads[0]
-    for angle in range(1, groups):
-        update = update + coeffs[angle][:, None, None] * grads[angle]
-    return ((slab - update)[None], misfit[0, 0])
+    )(path_lengths, jitter[:, 0, 0], step_sizes, *loaded)
+    return (volume - new, misfit[0, 0])
 
 
 def solution(mesh):

time: 41.5 us -> 37.1 us (0.89)
  Pallas kernels: 35.6 us -> 32.9 us
  local copies, waits for them, and re-layouts: 2.38 us -> 0.01 us
  other arithmetic: 0.86 us -> 1.65 us
    pallas_call x1, Pallas kernels: 35.6 us -> 32.9 us  [body(): pl.pallas_call(functools.partial(kernel, groups, columns, near), out_shap...]
    unnamed x6 -> x2, local copies, waits for them, and re-layouts: 1.36 us -> 0.01 us
    mul x2 -> x0, local copies, waits for them, and re-layouts: 1.02 us -> none  [body(): update = coeffs[0][:, None, None] * grads[0]]
    sub x1, other arithmetic: 0.79 us -> 1.65 us  [body(): return (volume - new, misfit[0, 0])]
where the time goes in v2:
time: 37.1 us; the launch traced here: 37 us
  Pallas kernels  32.9 us (89%)
  between operations  2.41 us (6%)
  other arithmetic  1.65 us (4%)
    pallas_call x1, Pallas kernels, body(): pl.pallas_call(functools.partial(kernel, groups, columns, near), out_shap...  32.9 us
    sub x1, other arithmetic, body(): return (volume - new, misfit[0, 0])  1.65 us

profile of v2, /device:TPU:0, one launch (start us, length us, event | category | flops | bytes accessed | tf_op | source)
XLA Modules:
  0.0 37.0 jit_solution(82076603236833552)
XLA Ops:
  0.6 0.0 copy-start
  0.6 32.9 %shard_map.113 = (f32[1,2,32,896]{3,2,1,0:T(8,128)}, f32[1,1]{1,0:T(1,128)}) custom-call(f32[2,2,2]{2,1,0:T(2,128)} %path_ref.1, s32[2,14]{1,0:T(2,128)} %bitcast.6, f32[2]{0:T(128)} %step_ref.1, f32[2,32,896]{2,1,0:T(8,128)} %bitcast.4, f32[2,128,128]{2,1,0:T(8,128)} %probe_hbm.1, bf16[14,128,128]{2,1,0:T(8,128)(2,1)} %bitcast.5, ...), custom_call_target="tpu_custom_call" | custom-call | tf_op jit(solution)/shard_map/pallas_call | solution.py:361
  33.5 0.0 copy-done
  33.5 1.7 %sub.3 = f32[1,2,32,896]{3,2,1,0:T(8,128)} subtract(f32[1,2,32,896]{3,2,1,0:T(8,128)S(1)} %copy-done, f32[1,2,32,896]{3,2,1,0:T(8,128)} %get-tuple-element.4) | non-fusion elementwise | flops 57344 | bytes 688128 | tf_op jit(solution)/shard_map/sub | solution.py:394
Async XLA Ops:
  0.6 32.9 %copy-start = (f32[1,2,32,896]{3,2,1,0:T(8,128)S(1)}, f32[1,2,32,896]{3,2,1,0:T(8,128)}, u32[]{:S(2)}) copy-start(f32[1,2,32,896]{3,2,1,0:T(8,128)} %param.10) | copy-start | bytes 688132

commit v3 on v2

--- a/solution.py
+++ b/solution.py
@@ -178,6 +178,33 @@
             def _():
                 fn(way)
 
+    odd = lax.rem(me, 2) == 1
+
+    def sent(fn):
+        for way, on in ((1, me + 1 < columns), (2, me >= 1), (0, ~odd & (me + 2 < columns)), (3, odd & (me >= 2))):
+            @pl.when(on)
+            def _():
+                fn(way)
+
+    def relayed(fn, tile):
+        for on, first, src, dst, send, way, device in (
+            (~odd & (me >= 2), 1, 32, 0, 3, 0, me + 1),
+            (odd & (me + 1 < columns), 2, 88, 120, 0, 3, me - 1),
+        ):
+            @pl.when(on)
+            def _():
+                fn(first, remote(
+                    ph.at[tile, pl.ds(src, 24)], ph.at[tile, pl.ds(dst, 24)],
+                    b_s.at[send, tile], b_r.at[way, tile], (group, device),
+                ))
+
+    def relay(tile):
+        def go(first, copy):
+            phase_copy(first, tile).wait_recv()
+            copy.start()
+
+        relayed(go, tile)
+
     for tile in range(tiles):
         for step in range(1, groups):
             angle_copy(step, tile).start()
@@ -188,7 +215,7 @@
             angle_copy(step, tile).wait_recv()
             own = own + arecv[step - 1, tile]
         ph[tile, OWN_FIRST : OWN_FIRST + rows] = own
-        ways(lambda way: phase_copy(way, tile).start(), 1)
+        sent(lambda way: phase_copy(way, tile).start())
         return carry
 
     lax.fori_loop(0, tiles, spread, 0)
@@ -198,7 +225,10 @@
     inside = (grid_row >= 0) & (grid_row < rows * columns)
 
     def prepare(tile):
-        ways(lambda way: phase_copy(way, tile).wait_recv(), -1)
+        for way, heard in ((0, me >= 2), (1, odd), (2, ~odd), (3, me + 2 < columns)):
+            @pl.when(heard)
+            def _():
+                phase_copy(way, tile).wait_recv()
         s, c = sin_cos(ph[tile])
         objr[tile + 1] = jnp.where(inside, c, 0.0)
         obji[tile + 1] = jnp.where(inside, s, 0.0)
@@ -286,12 +316,17 @@
     def far_copy(step):
         return remote(mis2.at[my_far], mis2.at[my_far], m2_s.at[step - 1], m2_r.at[step - 1], far_device(step))
 
+    relay(0)
+    relay(1)
     prepare(0)
+    relay(2)
     prepare(1)
     for load in loads[1:]:
         load.wait()
     misfit = forward(0)
     for p in range(tiles):
+        if p + 3 < tiles:
+            relay(p + 3)
         if p + 2 < tiles:
             prepare(p + 2)
         backward(p)
@@ -303,14 +338,16 @@
             mis1[near_id] = jnp.sum(misfit, axis=0, keepdims=True)
             for step in range(1, near_all):
                 near_copy(step).start()
-        if p >= 3:
-            finish(p - 3)
+        if p >= 5:
+            finish(p - 5)
     ways(lambda way: grad_copy(way, tiles - 1).start(), 1)
     for step in range(1, near_all):
         near_copy(step).wait_recv()
     mis2[my_far] = jnp.sum(mis1[...], axis=0)
     for step in range(1, far_count):
         far_copy(step).start()
+    finish(tiles - 5)
+    finish(tiles - 4)
     finish(tiles - 3)
     finish(tiles - 2)
     finish(tiles - 1)
@@ -319,7 +356,8 @@
         for step in range(1, groups):
             angle_copy(step, tile).wait_send()
             share_copy(step, tile).wait_send()
-        ways(lambda way: phase_copy(way, tile).wait_send(), 1)
+        sent(lambda way: phase_copy(way, tile).wait_send())
+        relayed(lambda first, copy: copy.wait_send(), tile)
         ways(lambda way: grad_copy(way, tile).wait_send(), 1)
         return carry
 

time: 37.1 us -> 34 us (0.916)
  Pallas kernels: 32.9 us -> 29.8 us
    pallas_call x1, Pallas kernels: 32.9 us -> 29.8 us  [body(): pl.pallas_call(functools.partial(kernel, groups, columns, near), out_shap...]
where the time goes in v3:
time: 34 us; the launch traced here: 33.8 us
  Pallas kernels  29.8 us (88%)
  between operations  2.41 us (7%)
  other arithmetic  1.65 us (5%)
    pallas_call x1, Pallas kernels, body(): pl.pallas_call(functools.partial(kernel, groups, columns, near), out_shap...  29.8 us
    sub x1, other arithmetic, body(): return (volume - new, misfit[0, 0])  1.65 us

profile of v3, /device:TPU:0, one launch (start us, length us, event | category | flops | bytes accessed | tf_op | source)
XLA Modules:
  0.0 33.8 jit_solution(12271325866168006086)
XLA Ops:
  0.6 0.0 copy-start
  0.6 29.8 %shard_map.113 = (f32[1,2,32,896]{3,2,1,0:T(8,128)}, f32[1,1]{1,0:T(1,128)}) custom-call(f32[2,2,2]{2,1,0:T(2,128)} %path_ref.1, s32[2,14]{1,0:T(2,128)} %bitcast.6, f32[2]{0:T(128)} %step_ref.1, f32[2,32,896]{2,1,0:T(8,128)} %bitcast.4, f32[2,128,128]{2,1,0:T(8,128)} %probe_hbm.1, bf16[14,128,128]{2,1,0:T(8,128)(2,1)} %bitcast.5, ...), custom_call_target="tpu_custom_call" | custom-call | tf_op jit(solution)/shard_map/pallas_call | solution.py:399
  30.4 0.0 copy-done
  30.4 1.7 %sub.3 = f32[1,2,32,896]{3,2,1,0:T(8,128)} subtract(f32[1,2,32,896]{3,2,1,0:T(8,128)S(1)} %copy-done, f32[1,2,32,896]{3,2,1,0:T(8,128)} %get-tuple-element.4) | non-fusion elementwise | flops 57344 | bytes 688128 | tf_op jit(solution)/shard_map/sub | solution.py:432
Async XLA Ops:
  0.6 29.8 %copy-start = (f32[1,2,32,896]{3,2,1,0:T(8,128)S(1)}, f32[1,2,32,896]{3,2,1,0:T(8,128)}, u32[]{:S(2)}) copy-start(f32[1,2,32,896]{3,2,1,0:T(8,128)} %param.10) | copy-start | bytes 688132
